TPU v7x, 256 devices: a whole 4x4x8 slice. The times are simulated.
256 devices in a mesh: span: 8 (over y, core), chord: 32 (over z, x).
Axes of the slice: x: 4, y: 4, z: 8, core: 2. Of those that a mesh axis runs over, the one named last changes fastest.
Arguments:
- node_pos: float32 [3, 524288], P(None, ('span', 'chord')), may hold values from -0.4 to 0.4
- ctrl_pos: float32 [3, 8192], P(None, ('span', 'chord')), may hold values from -0.4 to 0.4
- ctrl_ids: int32 [8192], P(('span', 'chord')), may hold values from 0 to 1023
- wing_shift: float32 [15, 1024], replicated, may hold values from -0.06 to 0.06
- wing_speed: float32 [15, 1024], replicated, may hold values from -0.6 to 0.6
- minv: float32 [8192, 8192], P(('span', 'chord')), may hold values from -1 to 3, as said below
- conn: int32 [64, 32768], P(None, ('span', 'chord')), may hold values from 0 to 2047
- face_elem: int32 [8, 32, 4, 32], P('span', 'chord'), may hold values from 0 to 127
- face_match: int32 [8, 32, 4, 32], P('span', 'chord'), may hold values from 0 to 31, each once within a row
Outputs:
- det_jac: float32 [5, 64, 32768], P(None, None, ('span', 'chord'))
- grid_flux: float32 [5, 3, 64, 32768], P(None, None, None, ('span', 'chord'))
- face_flux: float32 [8, 32, 4, 5, 16, 32], P('span', 'chord')
Inputs may be any that keep to these rules, and one draw needn't show every extreme that they name: minv is exactly symmetric. Each face_match[j, k, t, :] is a permutation of 0 to 31.
All inputs are finite; a program needn't handle non-finite values.
Results may differ from a plain program's by a relative error of at most 0.00025.
Values sent between devices are 32-bit elements; how exact they have to be, the bound alone decides.
A program may use at most 64 MiB of HBM per device.

v0:
```python
import math
import jax
import jax.numpy as jnp
import numpy as np
from jax import lax
from jax.sharding import Mesh
from jax.sharding import PartitionSpec as P

SPAN_CHORD = ("span_0", "span_1", "chord_0", "chord_1")
SPAN = ("span_0", "span_1")
CHORD = ("chord_0", "chord_1")
kernel_width = 0.1


def in_order(parts, dim):
    shape = list(parts.shape[1:])
    shape[dim] *= parts.shape[0]
    return jnp.moveaxis(parts, 0, dim).reshape(shape)


def stacked_from(shard, axes, sequence):
    parts = shard
    for k in sequence:
        parts = lax.all_gather(parts, axes[k])
    done = sequence[::-1]
    back = [done.index(k) for k in range(len(axes))]
    parts = parts.transpose(*back, *range(len(axes), parts.ndim))
    return parts.reshape(-1, *shard.shape)


def gather_axes(shard, axes, sequence, dim):
    return in_order(stacked_from(shard, axes, sequence), dim)


def gather_turned(arrays, axis, dims):
    turned = [jnp.moveaxis(a, dim, 0) for a, dim in zip(arrays, dims)]
    widths = [t[0].size for t in turned]
    both = jnp.concatenate([t.reshape(-1, w) for t, w in zip(turned, widths)], axis=1)
    whole = lax.all_gather(both, axis, axis=0, tiled=True)
    parts = jnp.split(whole, [sum(widths[:k]) for k in range(1, len(widths))], axis=1)
    return tuple(
        (
            jnp.moveaxis(b.reshape(-1, *t.shape[1:]), 0, dim)
            for b, t, dim in zip(parts, turned, dims)
        )
    )


def passed_along(block, axis, distance):
    devices = range(lax.axis_size(axis))
    route = [(i - distance, i) for i in devices if i - distance in devices]
    return lax.ppermute(block, axis, route)


def passed_along_2(value, axis, steps):
    count = lax.axis_size(axis)
    pairs = [(source, (source + steps) % count) for source in range(count)]
    return lax.ppermute(value, axis, pairs)


def lobatto_table():
    points = np.array([-1.0, -1.0 / np.sqrt(5.0), 1.0 / np.sqrt(5.0), 1.0])
    barycentric = np.array(
        [
            1.0
            / np.prod([points[target] - points[source] for source in range(4) if source != target])
            for target in range(4)
        ]
    )
    derivative = np.zeros((4, 4))
    for target in range(4):
        for source in range(4):
            if source != target:
                derivative[target, source] = (
                    barycentric[source] / barycentric[target] / (points[target] - points[source])
                )
        derivative[target, target] = -np.sum(derivative[target])
    identity = np.eye(4)
    stacked = np.stack(
        [
            np.kron(np.kron(derivative, identity), identity),
            np.kron(np.kron(identity, derivative), identity),
            np.kron(np.kron(identity, identity), derivative),
        ]
    )
    return stacked.reshape(192, 64)


def element_metrics(node_rows, positions, links):
    sections = node_rows.shape[0] // 6
    elements = links.shape[1]
    moved = node_rows[: 3 * sections] + jnp.tile(positions, (sections, 1))
    gathered = jnp.take(jnp.concatenate([moved, node_rows[3 * sections :]], axis=0), links, axis=1)
    table = jnp.asarray(lobatto_table(), jnp.float32)
    jacobian = jnp.einsum(
        "rq,kqe->rke", table, gathered[: 3 * sections], precision=lax.Precision.HIGHEST
    )
    jacobian = jacobian.reshape(3, 64, sections, 3, elements).transpose(2, 3, 0, 1, 4)
    velocity = gathered[3 * sections :].reshape(sections, 3, 64, elements)

    def entry(spatial, along):
        return jacobian[:, spatial % 3, along % 3]

    metric = [
        [
            entry(spatial + 1, along + 1) * entry(spatial + 2, along + 2)
            - entry(spatial + 1, along + 2) * entry(spatial + 2, along + 1)
            for spatial in range(3)
        ]
        for along in range(3)
    ]
    volume = entry(0, 0) * metric[0][0] + entry(0, 1) * metric[1][0] + entry(0, 2) * metric[2][0]
    flux = jnp.stack(
        [
            metric[along][0] * velocity[:, 0]
            + metric[along][1] * velocity[:, 1]
            + metric[along][2] * velocity[:, 2]
            for along in range(3)
        ],
        axis=1,
    )
    return (volume, flux)


def face_traces(flux, sides):
    sections, elements = (flux.shape[0], flux.shape[3])
    cube = flux.reshape(sections, 3, 4, 4, 4, elements)
    surfaces = [-cube[:, 2, :, :, 0], cube[:, 2, :, :, 3], -cube[:, 1, :, 0], cube[:, 1, :, 3]]
    return jnp.stack(
        [
            jnp.take(surface.reshape(sections, 16, elements), sides[ordinal], axis=2)
            for ordinal, surface in enumerate(surfaces)
        ]
    )


def kernel_sum(weights_piece, points_piece, nodes):
    columns = points_piece.shape[1]
    block_width = math.gcd(columns, 256)

    def step(counter, total):
        offset = counter * block_width
        weight_block = lax.dynamic_slice_in_dim(weights_piece, offset, block_width, 1)
        point_block = lax.dynamic_slice_in_dim(points_piece, offset, block_width, 1)
        distance = (
            (point_block[0][:, None] - nodes[0][None, :]) ** 2
            + (point_block[1][:, None] - nodes[1][None, :]) ** 2
            + (point_block[2][:, None] - nodes[2][None, :]) ** 2
        )
        kernel = jnp.exp(-distance / (2.0 * kernel_width**2))
        return total + jnp.dot(
            weight_block,
            kernel,
            precision=lax.Precision.HIGHEST,
            preferred_element_type=jnp.float32,
        )

    empty = jnp.zeros((weights_piece.shape[0], nodes.shape[1]), jnp.float32)
    return lax.fori_loop(0, columns // block_width, step, empty)


def on_device(
    node_pos, ctrl_pos, ctrl_ids, wing_shift, wing_speed, minv, conn, face_elem, face_match
):
    highest = lax.Precision.HIGHEST
    table = jnp.concatenate([wing_shift, wing_speed], axis=0)
    every_id = gather_axes(ctrl_ids, SPAN_CHORD, (0, 2, 3, 1), 0)
    right_side = jnp.take(table, every_id, axis=1)
    own_weights = lax.dot_general(
        right_side,
        minv,
        (((1,), (1,)), ((), ())),
        precision=highest,
        preferred_element_type=jnp.float32,
    )
    pieces = gather_turned((own_weights, ctrl_pos), SPAN_CHORD, (1, 1))
    motion = kernel_sum(pieces[0], pieces[1], node_pos)
    volume, flux = element_metrics(motion, node_pos, conn)
    own = face_traces(flux, face_elem[0, 0])
    lower = passed_along(own[1], SPAN, 1)
    upper = passed_along(own[0], SPAN, -1)
    before = passed_along_2(own[3], CHORD, 1)
    after = passed_along_2(own[2], CHORD, -1)
    received = jnp.stack([lower, upper, before, after])
    matched = jnp.stack(
        [jnp.take(received[ordinal], face_match[0, 0, ordinal], axis=2) for ordinal in range(4)]
    )
    position = lax.axis_index(SPAN)
    span_count = lax.axis_size(SPAN)
    side_index = jnp.arange(4, dtype=jnp.int32)
    boundary = (side_index == 0) & (position == 0) | (side_index == 1) & (
        position == span_count - 1
    )
    opposite = jnp.where(boundary[:, None, None, None], -own, matched)
    face_flux = (0.5 * (own - opposite))[None, None]
    return (volume, flux, face_flux)


def solution(mesh):
    split = Mesh(mesh.devices.reshape(4, 2, 8, 4), ("span_0", "span_1", "chord_0", "chord_1"))
    return jax.shard_map(
        on_device,
        mesh=split,
        in_specs=(
            P(None, SPAN_CHORD),
            P(None, SPAN_CHORD),
            P(SPAN_CHORD),
            P(),
            P(),
            P(SPAN_CHORD, None),
            P(None, SPAN_CHORD),
            P(SPAN, CHORD, None, None),
            P(SPAN, CHORD, None, None),
        ),
        out_specs=(
            P(None, None, SPAN_CHORD),
            P(None, None, None, SPAN_CHORD),
            P(SPAN, CHORD, None, None, None, None),
        ),
        check_vma=False,
    )
```

profile of v0, /device:TPU:1, one launch (start us, length us, event | category | flops | bytes accessed | tf_op | source)
XLA Modules:
  0.0 360.8 jit_solution(5451668358771411971)
XLA Ops:
  10.1 7.8 %all-reduce = s32[128]{0:T(128)S(1)} all-reduce(s32[128]{0:T(128)S(1)} %dynamic-update-slice), channel_id=2, replica_groups=mesh['span_0'=4,'span_1'=2,'chord_0'=8,'chord_1'=4] {'span_0'}, use_global_device_ids=true, to_apply=%add | all-reduce | flops 128 | bytes 1024
  18.0 19.8 %all-gather.4 = s32[8,4,32]{2,1,0:T(4,128)S(1)} all-gather(s32[1,4,32]{2,1,0:T(4,128)S(1)} %reshape.722), channel_id=3, replica_groups=mesh['span_0'=4,'span_1'=2,'chord_0'=8,'chord_1'=4] {'chord_0'}, dimensions={0}, use_global_device_ids=true | all-gather | bytes 4608 | tf_op jit(solution)/shard_map/all_gather | solution.py:24
  37.8 9.3 %all-gather.2 = s32[32,4,32]{2,1,0:T(4,128)S(1)} all-gather(s32[8,4,32]{2,1,0:T(4,128)S(1)} %all-gather.4), channel_id=4, replica_groups=mesh['span_0'=4,'span_1'=2,'chord_0'=8,'chord_1'=4] {'chord_1'}, dimensions={0}, use_global_device_ids=true | all-gather | bytes 20480 | tf_op jit(solution)/shard_map/all_gather | solution.py:24
  47.1 12.9 %all-gather.3 = s32[8,8,4,32]{3,1,2,0:T(8,128)S(1)} all-gather(s32[4,8,4,32]{3,1,2,0:T(8,128)S(1)} %copy.78), channel_id=5, replica_groups=mesh['span_0'=4,'span_1'=2,'chord_0'=8,'chord_1'=4] {'span_1'}, dimensions={0}, use_global_device_ids=true | all-gather | bytes 49152 | tf_op jit(solution)/shard_map/all_gather | solution.py:24
  61.6 27.7 %gather_fusion = f32[8192,30]{1,0:T(8,128)} fusion(f32[30,1024]{0,1:T(8,128)S(1)} %copy.81, s32[8192]{0:T(1024)S(1)} %broadcast_clamp_fusion), kind=kCustom, calls=%fused_computation.8 | custom fusion | bytes 1998848 | tf_op jit(solution)/shard_map/jit(_take)/gather | solution.py:168
  89.3 10.0 %fusion.25 = f32[32,30]{0,1:T(8,128)S(1)} fusion(f32[32,8192]{1,0:T(8,128)S(1)} %copy-done, f32[8192,30]{1,0:T(8,128)} %gather_fusion, pred[8192]{0:T(1024)(128)(4,1)S(1)} %compare_and_fusion), kind=kOutput, calls=%fused_computation.40 | convolution fusion | flops 94617600 | bytes 2043648 | tf_op jit(solution)/shard_map/dot_general | solution.py:169
  100.4 111.3 %all-gather.7.cloned.1.call-done = f32[8192,33]{1,0:T(8,128)} async-done(((f32[32,33]{1,0:T(8,128)}), f32[8192,33]{1,0:T(8,128)}) %all-gather.7.cloned.1.call-update) | async-done | bytes 1081360 | tf_op jit(solution)/shard_map/all_gather | solution.py:39
  211.7 5.3 %slice_bitcast_fusion = f32[3,8192]{0,1:T(8,128)} fusion(f32[8192,33]{1,0:T(8,128)} %all-gather.7.cloned.1.call-done), kind=kLoop, calls=%fused_computation.33 | loop fusion | bytes 196608 | tf_op jit(solution)/shard_map/transpose | solution.py:43
  217.1 2.8 copy.84
  219.9 4.5 %slice_bitcast_fusion.1 = f32[30,8192]{0,1:T(8,128)} fusion(f32[8192,33]{1,0:T(8,128)} %all-gather.7.cloned.1.call-done), kind=kLoop, calls=%fused_computation.34 | loop fusion | bytes 1966080 | tf_op jit(solution)/shard_map/transpose | solution.py:43
  224.4 2.9 copy.83
  227.2 71.6 %while.14 = (s32[]{:T(128)}, f32[30,2048]{1,0:T(8,128)S(1)}, f32[30,8192]{1,0:T(8,128)S(1)}, f32[3,8192]{1,0:T(4,128)S(1)}, f32[3,2048]{1,0:T(4,128)S(1)}, /*ind...) while((s32[]{:T(128)}, f32[30,2048]{1,0:T(8,128)S(1)}, ...), condition=%wide.region_1.2_spmd.clone, body=%wide.region_0.1_spmd.clone.sunk | while | flops 194109440 | bytes 623829 | solution.py:159
  229.6 2.1 convolution_add_fusion.2
  231.8 2.1 convolution_add_fusion.2
  240.8 2.1 convolution_add_fusion.2
  249.7 2.1 convolution_add_fusion.2
  258.7 2.1 convolution_add_fusion.2
  267.6 2.1 convolution_add_fusion.2
  294.5 2.1 convolution_add_fusion.2
  299.3 27.7 %gather_fusion.1 = f32[8192,30]{1,0:T(8,128)} fusion(f32[30,2048]{0,1:T(8,128)S(1)} %copy.85, s32[8192]{0:T(1024)S(1)} %bitcast_clamp_fusion), kind=kCustom, calls=%fused_computation.9 | custom fusion | bytes 1998848 | tf_op jit(solution)/shard_map/jit(_take)/gather | solution.py:93
  327.0 3.2 copy.113
  335.7 2.2 collective-permute-start.1
  338.9 3.4 collective-permute-start
  345.5 3.7 %collective-permute-start.3 = (f32[5,16,32]{1,0,2:T(8,128)S(1)}, f32[5,16,32]{1,0,2:T(8,128)S(1)}, u32[]{:S(2)}, u32[]{:S(2)}) collective-permute-start(f32[5,16,32]{1,0,2:T(8,128)S(1)} %get-tuple-element.172), channel_id=1, source_target_pairs={{0,31},{1,0},{2,1},{3,2},{4,3},{5,4},{6,5},{7,6},{8,7},{9,8},{10,9... | collective-permute-start | bytes 30728 | tf_op jit(solution)/shard_map/ppermute | solution.py:58
  (185 shorter events, 75.1 us)
Async XLA Ops:
  7.2 82.1 %copy-start = (f32[32,8192]{1,0:T(8,128)S(1)}, f32[32,8192]{1,0:T(8,128)}, u32[]{:S(2)}) copy-start(f32[32,8192]{1,0:T(8,128)} %param.21) | copy-start | bytes 3145732
  7.2 204.5 %all-gather.7.cloned.1.call-start = ((), (), s32[]{:S(2)}) async-start(), calls=%async_computation | async-start | bytes 4210688 | tf_op jit(solution)/shard_map/all_gather | solution.py:39
  89.3 10.0 %copy-start.4 = (f32[3,32]{1,0:T(4,128)S(1)}, f32[3,32]{1,0:T(4,128)}, u32[]{:S(2)}) copy-start(f32[3,32]{1,0:T(4,128)} %param.17) | copy-start | bytes 1156
  89.3 10.8 %copy-start.1 = (f32[3,2048]{1,0:T(4,128)S(1)}, f32[3,2048]{1,0:T(4,128)}, u32[]{:S(2)}) copy-start(f32[3,2048]{1,0:T(4,128)} %param.16) | copy-start | bytes 73732
  89.3 10.9 %copy-start.5 = (s32[1,1,4,32]{3,2,1,0:T(4,128)S(1)}, s32[1,1,4,32]{3,2,1,0:T(4,128)}, u32[]{:S(2)}) copy-start(s32[1,1,4,32]{3,2,1,0:T(4,128)} %param.23) | copy-start | bytes 1540
  89.3 11.0 %copy-start.6 = (s32[1,1,4,32]{3,2,1,0:T(4,128)S(1)}, s32[1,1,4,32]{3,2,1,0:T(4,128)}, u32[]{:S(2)}) copy-start(s32[1,1,4,32]{3,2,1,0:T(4,128)} %param.24) | copy-start | bytes 1540
  89.3 11.0 %copy-start.2 = (s32[64,128]{1,0:T(8,128)S(1)}, s32[64,128]{1,0:T(8,128)}, u32[]{:S(2)}) copy-start(s32[64,128]{1,0:T(8,128)} %param.22) | copy-start | bytes 98308
  330.2 0.8 copy-start.3
  335.7 13.6 %collective-permute-start.1 = (f32[5,16,32]{1,0,2:T(8,128)S(1)}, f32[5,16,32]{1,0,2:T(8,128)S(1)}, u32[]{:S(2)}, u32[]{:S(2)}) collective-permute-start(f32[5,16,32]{1,0,2:T(8,128)S(1)} %get-tuple-element.168), channel_id=1, source_target_pairs={{32,0},{64,32},{96,64},{128,96},{160,128},{192,160},{224,192},{33,... | collective-permute-start | bytes 30728 | tf_op jit(solution)/shard_map/ppermute | solution.py:52
  338.9 11.0 %collective-permute-start = (f32[5,16,32]{1,0,2:T(8,128)S(1)}, f32[5,16,32]{1,0,2:T(8,128)S(1)}, u32[]{:S(2)}, u32[]{:S(2)}) collective-permute-start(f32[5,16,32]{1,0,2:T(8,128)S(1)} %get-tuple-element.170), channel_id=1, source_target_pairs={{0,32},{32,64},{64,96},{96,128},{128,160},{160,192},{192,224},{1,3... | collective-permute-start | bytes 30728 | tf_op jit(solution)/shard_map/ppermute | solution.py:52
  343.3 8.1 %collective-permute-start.2 = (f32[5,16,32]{1,0,2:T(8,128)S(1)}, f32[5,16,32]{1,0,2:T(8,128)S(1)}, u32[]{:S(2)}, u32[]{:S(2)}) collective-permute-start(f32[5,16,32]{1,0,2:T(8,128)S(1)} %get-tuple-element.174), channel_id=1, source_target_pairs={{0,1},{1,2},{2,3},{3,4},{4,5},{5,6},{6,7},{7,8},{8,9},{9,10},{10,1... | collective-permute-start | bytes 30728 | tf_op jit(solution)/shard_map/ppermute | solution.py:58
  345.5 6.9 %collective-permute-start.3 = (f32[5,16,32]{1,0,2:T(8,128)S(1)}, f32[5,16,32]{1,0,2:T(8,128)S(1)}, u32[]{:S(2)}, u32[]{:S(2)}) collective-permute-start(f32[5,16,32]{1,0,2:T(8,128)S(1)} %get-tuple-element.172), channel_id=1, source_target_pairs={{0,31},{1,0},{2,1},{3,2},{4,3},{5,4},{6,5},{7,6},{8,7},{9,8},{10,9... | collective-permute-start | bytes 30728 | tf_op jit(solution)/shard_map/ppermute | solution.py:58
Sparse Core Ops, SparseCore 0:
  100.2 111.5 all-gather.6
where the time goes:
time: 361 us
  waiting for transfers between devices  112 us (31%)
  local copies, waits for them, and re-layouts  88.7 us (25%)
  matrix products  78.6 us (22%)
  blocking collectives  49.8 us (14%)
  between operations  15.3 us (4%)
  starting transfers between devices  10.5 us (3%)
  other arithmetic  4.66 us (1%)
    all_gather x1, waiting for transfers between devices, gather_turned(): whole = lax.all_gather(both, axis, axis=0, tiled=True)  111 us
    dot_general x32, matrix products, step(): jnp.dot(weight_block, kernel, precision=lax.Precision.HIGHEST, preferred_...  67.3 us
    all_gather x3, blocking collectives, stacked_from(): parts = lax.all_gather(parts, axes[k])  42 us
    gather x2, local copies, waits for them, and re-layouts, element_metrics(): jnp.take(jnp.concatenate([moved, node_rows[3 * sections:]], axis=0), link...  30.9 us
    gather x1, local copies, waits for them, and re-layouts, on_device(): right_side = jnp.take(table, every_id, axis=1)  27.7 us
    dot_general x1, matrix products, on_device(): lax.dot_general(right_side, minv, (((1,), (1,)), ((), ())), precision=hig...  9.97 us
    transpose x2, local copies, waits for them, and re-layouts, gather_turned(): jnp.moveaxis(b.reshape(-1, *t.shape[1:]), 0, dim)  9.81 us
    unnamed x20, local copies, waits for them, and re-layouts  8.74 us
  transfers between devices with their start and end apart: 5, of which 2 were waited for; matrix products, arithmetic and copies ran while one was open for 2% of the time, Pallas kernels for 0%

commit v1 on v0

--- a/solution.py
+++ b/solution.py
@@ -10,6 +10,15 @@
 SPAN = ("span_0", "span_1")
 CHORD = ("chord_0", "chord_1")
 kernel_width = 0.1
+_choose_counts = lambda body, comm_axis, on_dim: jnp.concatenate(
+    lax.all_to_all(
+        jnp.stack([body for _ in range(lax.axis_size(comm_axis))]),
+        axis_name=comm_axis,
+        split_axis=0,
+        concat_axis=0,
+    ),
+    axis=on_dim,
+)
 
 
 def in_order(parts, dim):
@@ -36,7 +45,7 @@
     turned = [jnp.moveaxis(a, dim, 0) for a, dim in zip(arrays, dims)]
     widths = [t[0].size for t in turned]
     both = jnp.concatenate([t.reshape(-1, w) for t, w in zip(turned, widths)], axis=1)
-    whole = lax.all_gather(both, axis, axis=0, tiled=True)
+    whole = _choose_counts(both, axis, 0)
     parts = jnp.split(whole, [sum(widths[:k]) for k in range(1, len(widths))], axis=1)
     return tuple(
         (

time: 361 us -> 292 us (0.81)
  waiting for transfers between devices: 112 us -> 32.9 us
  between operations: 15.3 us -> 1.9 us
  local copies, waits for them, and re-layouts: 88.7 us -> 101 us
  starting transfers between devices: 10.5 us -> 18 us
    all_gather x1 -> x0, waiting for transfers between devices: 111 us -> none  [gather_turned(): whole = lax.all_gather(both, axis, axis=0, tiled=True)]
    all_to_all x0 -> x1, waiting for transfers between devices: none -> 32.9 us  [lax.all_to_all(jnp.stack([body for _ in range(lax.axis_size(comm_axis))])...]
    unnamed x20 -> x26, local copies, waits for them, and re-layouts: 8.74 us -> 22.9 us
    transpose x2 -> x0, local copies, waits for them, and re-layouts: 9.81 us -> none  [gather_turned(): jnp.moveaxis(b.reshape(-1, *t.shape[1:]), 0, dim)]
    all_to_all x0 -> x1, starting transfers between devices: none -> 7.24 us  [lax.all_to_all(jnp.stack([body for _ in range(lax.axis_size(comm_axis))])...]
    split x0 -> x1, local copies, waits for them, and re-layouts: none -> 5.33 us  [gather_turned(): jnp.split(whole, [sum(widths[:k]) for k in range(1, len(widths))], axis=1)]
  transfers between devices with their start and end apart: 5 -> 5, of which waited for: 2 -> 1; matrix products, arithmetic and copies ran while one was open for 2% -> 2% of each run, Pallas kernels for 0% -> 0%
where the time goes in v1:
time: 292 us
  local copies, waits for them, and re-layouts  101 us (35%)
  matrix products  78.6 us (27%)
  blocking collectives  49.8 us (17%)
  waiting for transfers between devices  32.9 us (11%)
  starting transfers between devices  18 us (6%)
  other arithmetic  8.1 us (3%)
    dot_general x32, matrix products, step(): jnp.dot(weight_block, kernel, precision=lax.Precision.HIGHEST, preferred_...  67.3 us
    all_gather x3, blocking collectives, stacked_from(): parts = lax.all_gather(parts, axes[k])  42 us
    all_to_all x1, waiting for transfers between devices, lax.all_to_all(jnp.stack([body for _ in range(lax.axis_size(comm_axis))])...  32.9 us
    gather x2, local copies, waits for them, and re-layouts, element_metrics(): jnp.take(jnp.concatenate([moved, node_rows[3 * sections:]], axis=0), link...  30.8 us
    gather x1, local copies, waits for them, and re-layouts, on_device(): right_side = jnp.take(table, every_id, axis=1)  27.8 us
    unnamed x26, local copies, waits for them, and re-layouts  22.9 us
    dot_general x1, matrix products, on_device(): lax.dot_general(right_side, minv, (((1,), (1,)), ((), ())), precision=hig...  9.95 us
    unnamed x1, blocking collectives  7.85 us
  transfers between devices with their start and end apart: 5, of which 1 were waited for; matrix products, arithmetic and copies ran while one was open for 2% of the time, Pallas kernels for 0%

profile of v1, /device:TPU:1, one launch (start us, length us, event | category | flops | bytes accessed | tf_op | source)
XLA Modules:
  0.0 291.9 jit_solution(9548399872651170710)
XLA Ops:
  3.5 7.8 %all-reduce = s32[128]{0:T(128)S(1)} all-reduce(s32[128]{0:T(128)S(1)} %dynamic-update-slice), channel_id=2, replica_groups=mesh['span_0'=4,'span_1'=2,'chord_0'=8,'chord_1'=4] {'span_0'}, use_global_device_ids=true, to_apply=%add | all-reduce | flops 128 | bytes 1024
  11.5 19.8 %all-gather.4 = s32[8,4,32]{2,1,0:T(4,128)S(1)} all-gather(s32[1,4,32]{2,1,0:T(4,128)S(1)} %reshape.728), channel_id=3, replica_groups=mesh['span_0'=4,'span_1'=2,'chord_0'=8,'chord_1'=4] {'chord_0'}, dimensions={0}, use_global_device_ids=true | all-gather | bytes 4608 | tf_op jit(solution)/shard_map/all_gather | solution.py:33
  31.2 9.3 %all-gather.2 = s32[32,4,32]{2,1,0:T(4,128)S(1)} all-gather(s32[8,4,32]{2,1,0:T(4,128)S(1)} %all-gather.4), channel_id=4, replica_groups=mesh['span_0'=4,'span_1'=2,'chord_0'=8,'chord_1'=4] {'chord_1'}, dimensions={0}, use_global_device_ids=true | all-gather | bytes 20480 | tf_op jit(solution)/shard_map/all_gather | solution.py:33
  40.6 12.9 %all-gather.3 = s32[8,8,4,32]{3,1,2,0:T(8,128)S(1)} all-gather(s32[4,8,4,32]{3,1,2,0:T(8,128)S(1)} %copy.78), channel_id=5, replica_groups=mesh['span_0'=4,'span_1'=2,'chord_0'=8,'chord_1'=4] {'span_1'}, dimensions={0}, use_global_device_ids=true | all-gather | bytes 49152 | tf_op jit(solution)/shard_map/all_gather | solution.py:33
  55.0 27.8 %gather_fusion = f32[8192,30]{1,0:T(8,128)} fusion(f32[30,1024]{0,1:T(8,128)S(1)} %copy.81, s32[8192]{0:T(1024)S(1)} %broadcast_clamp_fusion), kind=kCustom, calls=%fused_computation.8 | custom fusion | bytes 1998848 | tf_op jit(solution)/shard_map/jit(_take)/gather | solution.py:177
  82.8 9.9 %fusion.25 = f32[32,30]{0,1:T(8,128)S(1)} fusion(f32[32,8192]{1,0:T(8,128)S(1)} %copy-done, f32[8192,30]{1,0:T(8,128)} %gather_fusion, pred[8192]{0:T(1024)(128)(4,1)S(1)} %compare_and_fusion), kind=kOutput, calls=%fused_computation.38 | convolution fusion | flops 94617600 | bytes 2043648 | tf_op jit(solution)/shard_map/dot_general | solution.py:178
  92.8 2.5 stack.28
  95.3 7.3 %reshape.751 = f32[256,1,1056]{2,1,0:T(1,128)} reshape(f32[256,32,33]{2,1,0:T(8,128)} %stack.28) | data formatting | bytes 2162688
  102.7 7.2 %all-to-all-start = ((f32[256,1,1056]{2,1,0:T(1,128)}), f32[256,1,1056]{2,1,0:T(1,128)S(1)}, u32[]{:S(2)}, u32[]{:S(2)}) async-start(f32[256,1,1056]{2,1,0:T(1,128)} %reshape.751), calls=%async_computation | async-start | bytes 2359296 | tf_op jit(solution)/shard_map/all_to_all | solution.py:14
  110.9 32.9 %all-to-all-done = f32[256,1,1056]{2,1,0:T(1,128)S(1)} async-done(((f32[256,1,1056]{2,1,0:T(1,128)}), f32[256,1,1056]{2,1,0:T(1,128)S(1)}, u32[]{:S(2)}, u32[]{:S(2)}) %all-to-all-start) | async-done | bytes 1081376 | tf_op jit(solution)/shard_map/all_to_all | solution.py:14
  144.3 3.4 %reduce = f32[256,1056]{1,0:T(8,128)S(1)} reduce(f32[256,1,1056]{2,1,0:T(1,128)S(1)} %all-to-all-done, f32[]{:T(128)} %broadcast.222), dimensions={1}, to_apply=%all_to_all.3.reduce_sub_computation | reduce | bytes 2162692 | tf_op jit(solution)/shard_map/all_to_all | solution.py:14
  147.8 6.8 %reshape.752 = f32[256,32,33]{2,1,0:T(8,128)} reshape(f32[256,1056]{1,0:T(8,128)S(1)} %reduce) | data formatting | bytes 2162688
  154.5 5.3 %split.9 = f32[8192,3]{1,0:T(8,128)} slice(f32[8192,33]{1,0:T(8,128)} %bitcast.183), slice={[0:8192], [30:33]} | slice | bytes 196608 | tf_op jit(solution)/shard_map/split | solution.py:49
  159.8 2.8 copy.115
  162.7 2.9 copy.114
  165.6 71.7 %while.14 = (s32[]{:T(128)}, f32[30,2048]{1,0:T(8,128)S(1)}, f32[30,8192]{1,0:T(8,128)S(1)}, f32[3,8192]{1,0:T(4,128)S(1)}, f32[3,2048]{1,0:T(4,128)S(1)}, /*ind...) while((s32[]{:T(128)}, f32[30,2048]{1,0:T(8,128)S(1)}, ...), condition=%wide.region_1.2_spmd.clone, body=%wide.region_0.1_spmd.clone.sunk | while | flops 194109440 | bytes 623821 | solution.py:168
  168.0 2.1 convolution_add_fusion.2
  170.2 2.1 convolution_add_fusion.2
  172.5 2.1 convolution_add_fusion.2
  174.7 2.1 convolution_add_fusion.2
  237.8 27.8 %gather_fusion.1 = f32[8192,30]{1,0:T(8,128)} fusion(f32[30,2048]{0,1:T(8,128)S(1)} %copy.84, s32[8192]{0:T(1024)S(1)} %bitcast_clamp_fusion), kind=kCustom, calls=%fused_computation.9 | custom fusion | bytes 1998848 | tf_op jit(solution)/shard_map/jit(_take)/gather | solution.py:102
  265.5 3.1 %copy.113 = f32[64,128,30]{1,0,2:T(8,128)S(1)} copy(f32[64,128,30]{2,1,0:T(8,128)} %bitcast.188) | data formatting | bytes 1966080 | tf_op jit(solution)/shard_map/jit(_take)/gather | solution.py:102
  276.2 3.7 %collective-permute-start = (f32[5,16,32]{1,0,2:T(8,128)S(1)}, f32[5,16,32]{1,0,2:T(8,128)S(1)}, u32[]{:S(2)}, u32[]{:S(2)}) collective-permute-start(f32[5,16,32]{1,0,2:T(8,128)S(1)} %get-tuple-element.165), channel_id=1, source_target_pairs={{0,32},{32,64},{64,96},{96,128},{128,160},{160,192},{192,224},{1,3... | collective-permute-start | bytes 30728 | tf_op jit(solution)/shard_map/ppermute | solution.py:61
  282.6 4.1 %collective-permute-start.3 = (f32[5,16,32]{1,0,2:T(8,128)S(1)}, f32[5,16,32]{1,0,2:T(8,128)S(1)}, u32[]{:S(2)}, u32[]{:S(2)}) collective-permute-start(f32[5,16,32]{1,0,2:T(8,128)S(1)} %get-tuple-element.167), channel_id=1, source_target_pairs={{0,31},{1,0},{2,1},{3,2},{4,3},{5,4},{6,5},{7,6},{8,7},{9,8},{10,9... | collective-permute-start | bytes 30728 | tf_op jit(solution)/shard_map/ppermute | solution.py:67
  (192 shorter events, 83.0 us)
Async XLA Ops:
  0.6 82.2 %copy-start = (f32[32,8192]{1,0:T(8,128)S(1)}, f32[32,8192]{1,0:T(8,128)}, u32[]{:S(2)}) copy-start(f32[32,8192]{1,0:T(8,128)} %param.21) | copy-start | bytes 3145732
  82.8 10.0 %copy-start.6 = (f32[3,32]{1,0:T(4,128)S(1)}, f32[3,32]{1,0:T(4,128)}, u32[]{:S(2)}) copy-start(f32[3,32]{1,0:T(4,128)} %param.17) | copy-start | bytes 1156
  102.6 7.3 %copy-start.1 = (f32[3,2048]{1,0:T(4,128)S(1)}, f32[3,2048]{1,0:T(4,128)}, u32[]{:S(2)}) copy-start(f32[3,2048]{1,0:T(4,128)} %param.16) | copy-start | bytes 73732
  102.6 8.0 %copy-start.7 = (s32[1,1,4,32]{3,2,1,0:T(4,128)S(1)}, s32[1,1,4,32]{3,2,1,0:T(4,128)}, u32[]{:S(2)}) copy-start(s32[1,1,4,32]{3,2,1,0:T(4,128)} %param.23) | copy-start | bytes 1540
  102.6 8.1 %copy-start.8 = (s32[1,1,4,32]{3,2,1,0:T(4,128)S(1)}, s32[1,1,4,32]{3,2,1,0:T(4,128)}, u32[]{:S(2)}) copy-start(s32[1,1,4,32]{3,2,1,0:T(4,128)} %param.24) | copy-start | bytes 1540
  102.6 8.2 %copy-start.4 = (s32[64,128]{1,0:T(8,128)S(1)}, s32[64,128]{1,0:T(8,128)}, u32[]{:S(2)}) copy-start(s32[64,128]{1,0:T(8,128)} %param.22) | copy-start | bytes 98308
  102.7 41.1 %all-to-all-start = ((f32[256,1,1056]{2,1,0:T(1,128)}), f32[256,1,1056]{2,1,0:T(1,128)S(1)}, u32[]{:S(2)}, u32[]{:S(2)}) async-start(f32[256,1,1056]{2,1,0:T(1,128)} %reshape.751), calls=%async_computation | async-start | bytes 2359296 | tf_op jit(solution)/shard_map/all_to_all | solution.py:14
  162.7 2.9 %copy-start.3 = (f32[30,2048]{1,0:T(8,128)S(1)}, f32[30,2048]{1,0:T(8,128)}, u32[]{:S(2)}) copy-start(f32[30,2048]{1,0:T(8,128)} %custom-call) | copy-start | bytes 737284
  165.6 71.7 %copy-start.2 = (f32[15,2048]{1,0:T(8,128)S(1)}, f32[15,2048]{1,0:T(8,128)}, u32[]{:S(2)}) copy-start(f32[15,2048]{1,0:T(8,128)} %tile.10) | copy-start | bytes 368644
  268.6 0.8 copy-start.5
  273.1 14.8 %collective-permute-start.1 = (f32[5,16,32]{1,0,2:T(8,128)S(1)}, f32[5,16,32]{1,0,2:T(8,128)S(1)}, u32[]{:S(2)}, u32[]{:S(2)}) collective-permute-start(f32[5,16,32]{1,0,2:T(8,128)S(1)} %get-tuple-element.163), channel_id=1, source_target_pairs={{32,0},{64,32},{96,64},{128,96},{160,128},{192,160},{224,192},{33,... | collective-permute-start | bytes 30728 | tf_op jit(solution)/shard_map/ppermute | solution.py:61
  276.2 12.4 %collective-permute-start = (f32[5,16,32]{1,0,2:T(8,128)S(1)}, f32[5,16,32]{1,0,2:T(8,128)S(1)}, u32[]{:S(2)}, u32[]{:S(2)}) collective-permute-start(f32[5,16,32]{1,0,2:T(8,128)S(1)} %get-tuple-element.165), channel_id=1, source_target_pairs={{0,32},{32,64},{64,96},{96,128},{128,160},{160,192},{192,224},{1,3... | collective-permute-start | bytes 30728 | tf_op jit(solution)/shard_map/ppermute | solution.py:61
  280.8 8.5 %collective-permute-start.2 = (f32[5,16,32]{1,0,2:T(8,128)S(1)}, f32[5,16,32]{1,0,2:T(8,128)S(1)}, u32[]{:S(2)}, u32[]{:S(2)}) collective-permute-start(f32[5,16,32]{1,0,2:T(8,128)S(1)} %get-tuple-element.169), channel_id=1, source_target_pairs={{0,1},{1,2},{2,3},{3,4},{4,5},{5,6},{6,7},{7,8},{8,9},{9,10},{10,1... | collective-permute-start | bytes 30728 | tf_op jit(solution)/shard_map/ppermute | solution.py:67
  282.6 7.7 %collective-permute-start.3 = (f32[5,16,32]{1,0,2:T(8,128)S(1)}, f32[5,16,32]{1,0,2:T(8,128)S(1)}, u32[]{:S(2)}, u32[]{:S(2)}) collective-permute-start(f32[5,16,32]{1,0,2:T(8,128)S(1)} %get-tuple-element.167), channel_id=1, source_target_pairs={{0,31},{1,0},{2,1},{3,2},{4,3},{5,4},{6,5},{7,6},{8,7},{9,8},{10,9... | collective-permute-start | bytes 30728 | tf_op jit(solution)/shard_map/ppermute | solution.py:67
